TPU v7x, 32 devices: a whole 2x2x4 slice. The times are simulated.
32 devices in a mesh: cuts: 16 (over z, y, x), circ: 2 (over core).
Axes of the slice: x: 2, y: 2, z: 4, core: 2. Of those that a mesh axis runs over, the one named last changes fastest.
Arguments:
- sources: bfloat16 [16, 8, 2, 16, 1024], P('cuts', None, 'circ'), may hold values from -6 to 6
- block_inverse: bfloat16 [2, 1024, 1024], P('circ'), may hold values from -0.0115625 to 0.92
- memory_factor: float32 [16, 2, 1024], P('cuts', 'circ'), may hold values from 0.5 to 1
- coupling_target: int32 [2, 4], P('circ'), may hold values from 0 to 1, as said below
- coupling_weight: bfloat16 [2, 4, 128, 1024], P('circ'), may hold values from -0.09375 to 0.09375
- coarse_decay: float32 [16, 2, 1024], P('cuts', 'circ'), may hold values from 0.2 to 0.995
- initial_state: float32 [2, 16, 1024], P('circ'), may hold values from -6 to 6
Outputs:
- slice_starts: float32 [16, 2, 16, 1024], P('cuts', 'circ')
- waveform: bfloat16 [16, 8, 2, 16, 1024], P('cuts', None, 'circ')
Inputs may be any that keep to these rules, and one draw needn't show every extreme that they name: `coupling_target`: row j names 4 subcircuits, j itself among them possibly; a row may name one subcircuit twice.
All inputs are finite; a program needn't handle non-finite values.
Results may differ from a plain program's by a relative error of at most 0.007.
Values sent between devices are 32-bit elements; how exact they have to be, the bound alone decides.
A program may use at most 64 MiB of HBM per device.

v0:
```python
import jax
import jax.numpy as jnp
from jax import lax
from jax.sharding import PartitionSpec as P

SWEEPS = 3
ITERS = 2


def carried_in(part, axis, combine, identity):
    place = lax.axis_index(axis)
    gathered = jax.tree.map(lambda a: lax.all_gather(a, axis), part)
    state = jax.tree.map(lambda a, e: jnp.zeros_like(a) + jnp.asarray(e, a.dtype), part, identity)

    def one(turn, state):
        return combine(
            state, jax.tree.map(lambda a: lax.dynamic_index_in_dim(a, turn, 0, False), gathered)
        )

    return lax.fori_loop(0, place, one, state)


def run_chain(decay_rate, coarse_terms, initial):

    def compose(earlier, latter):
        return (earlier[0] * latter[0], latter[0] * earlier[1] + latter[1])

    identity = (jnp.ones_like(decay_rate), jnp.zeros_like(coarse_terms))
    total_decay, total_terms = carried_in((decay_rate, coarse_terms), "cuts", compose, identity)
    return total_decay * initial + total_terms


def shards(
    sources,
    block_inverse,
    memory_factor,
    coupling_target,
    coupling_weight,
    coarse_decay,
    initial_state,
):
    own_sources = sources[0]
    factor = memory_factor[0][:, None, :]
    decay_rate = coarse_decay[0][:, None, :]
    local_subs = block_inverse.shape[0]
    every_sub = local_subs * lax.axis_size("circ")
    port_count = coupling_weight.shape[2]
    steps_count = own_sources.shape[0]
    owners = (
        coupling_target[:, :, None] == jnp.arange(every_sub, dtype=jnp.int32)[None, None, :]
    ).astype(jnp.float32)
    coarse_load = jnp.mean(own_sources.astype(jnp.float32), axis=0)
    begin_state = run_chain(decay_rate, coarse_load, initial_state)
    wave_now = None
    for iteration in range(ITERS):
        wave_now = jnp.broadcast_to(begin_state, (steps_count,) + begin_state.shape)
        for sweep_index in range(SWEEPS):
            sweep_wave_low = wave_now.astype(jnp.bfloat16)
            inflow = lax.psum_scatter(
                jnp.einsum(
                    "skg,sktqp->gtqp",
                    owners,
                    jnp.einsum(
                        "skpn,tsqn->sktqp",
                        coupling_weight,
                        sweep_wave_low,
                        preferred_element_type=jnp.float32,
                    ),
                    precision=lax.Precision.HIGHEST,
                ),
                "circ",
                scatter_dimension=0,
                tiled=True,
            )
            previous = begin_state
            columns = []
            for step_index in range(steps_count):
                drive_term = factor * previous + own_sources[step_index].astype(jnp.float32)
                drive_term = drive_term.at[:, :, :port_count].add(inflow[:, step_index])
                previous = jnp.einsum(
                    "smn,sqn->sqm",
                    block_inverse,
                    drive_term.astype(jnp.bfloat16),
                    preferred_element_type=jnp.float32,
                )
                columns.append(previous)
            wave_now = jnp.stack(columns)
        correction = wave_now[-1] - decay_rate * begin_state
        begin_state = run_chain(decay_rate, correction, initial_state)
    return (begin_state[None], wave_now.astype(jnp.bfloat16)[None])


def solution(mesh):
    return jax.shard_map(
        shards,
        mesh=mesh,
        in_specs=(
            P("cuts", None, "circ", None, None),
            P("circ", None, None),
            P("cuts", "circ", None),
            P("circ", None),
            P("circ", None, None, None),
            P("cuts", "circ", None),
            P("circ", None, None),
        ),
        out_specs=(P("cuts", "circ", None, None), P("cuts", None, "circ", None, None)),
        check_vma=False,
    )
```

profile of v0, /device:TPU:28, one launch (start us, length us, event | category | flops | bytes accessed | tf_op | source)
XLA Modules:
  0.0 464.5 jit_solution(4362443479391078707)
XLA Ops:
  9.1 35.0 %all-gather = f32[16,1,1024]{2,1,0:T(1,128)S(1)} all-gather(f32[1,1,1024]{2,1,0:T(1,128)} %param.114), channel_id=2, replica_groups=mesh['cuts'=16,'circ'=2] {'cuts'}, dimensions={0}, use_global_device_ids=true | all-gather | bytes 69632 | tf_op jit(solution)/shard_map/all_gather | solution.py:12
  44.1 22.1 %all-gather.8.cloned.1.call-done = f32[256,1024]{1,0:T(8,128)} async-done(((f32[16,1024]{1,0:T(8,128)}), f32[256,1024]{1,0:T(8,128)}) %all-gather.8.cloned.1.call-update) | async-done | bytes 1048592 | tf_op jit(solution)/shard_map/all_gather | solution.py:12
  66.3 12.8 %while.84 = (s32[]{:T(128)}, f32[1,1,1024]{2,1,0:T(1,128)S(1)}, f32[1,16,1024]{2,1,0:T(8,128)S(1)}, s32[]{:T(128)}, f32[16,1,1,1024]{3,2,1,0:T(1,128)S(1)}, /*in...) while((s32[]{:T(128)}, f32[1,1,1024]{2,1,0:T(1,128)S(1)}, f32[1,16,1024]{2,1,0:T(8,128)S(1)}, ...), condition=%wide.region_2.3_spmd, body=%wide.region_1.2_spmd.sunk | while | flops 33797 | bytes 217231 | solution.py:20
  82.6 8.0 %reduce-scatter.7.cloned.1.call-done = f32[1,8,16,128]{3,2,1,0:T(8,128)} async-done(((f32[2,8,16,128]{3,2,1,0:T(8,128)}), f32[1,8,16,128]{3,2,1,0:T(8,128)}) %reduce-scatter.7.cloned.1.call-update) | async-done | bytes 65552 | tf_op jit(solution)/shard_map/reduce_scatter | solution.py:59
  94.6 1.5 constant_dynamic-update-slice_fusion.5
  98.8 1.5 constant_dynamic-update-slice_fusion.4
  101.7 1.3 constant_dynamic-update-slice_fusion.80
  103.1 1.5 constant_dynamic-update-slice_fusion.3
  107.3 1.5 constant_dynamic-update-slice_fusion.2
  111.5 1.5 constant_dynamic-update-slice_fusion.1
  114.4 1.3 constant_dynamic-update-slice_fusion.77
  115.7 1.5 constant_dynamic-update-slice_fusion
  119.9 1.5 fusion.177
  123.1 8.8 %reduce-scatter.9.cloned.1.call-done = f32[1,8,16,128]{3,2,1,0:T(8,128)} async-done(((f32[2,8,16,128]{3,2,1,0:T(8,128)}), f32[1,8,16,128]{3,2,1,0:T(8,128)}) %reduce-scatter.9.cloned.1.call-update) | async-done | bytes 65552 | tf_op jit(solution)/shard_map/reduce_scatter | solution.py:59
  136.0 1.5 constant_dynamic-update-slice_fusion.12
  140.2 1.5 constant_dynamic-update-slice_fusion.11
  143.1 1.3 constant_dynamic-update-slice_fusion.72
  144.4 1.5 constant_dynamic-update-slice_fusion.10
  148.6 1.5 constant_dynamic-update-slice_fusion.9
  152.8 1.5 constant_dynamic-update-slice_fusion.8
  157.0 1.5 constant_dynamic-update-slice_fusion.7
  161.2 1.5 fusion.171
  164.7 8.6 %reduce-scatter.11.cloned.1.call-done = f32[1,8,16,128]{3,2,1,0:T(8,128)} async-done(((f32[2,8,16,128]{3,2,1,0:T(8,128)}), f32[1,8,16,128]{3,2,1,0:T(8,128)}) %reduce-scatter.11.cloned.1.call-update) | async-done | bytes 65552 | tf_op jit(solution)/shard_map/reduce_scatter | solution.py:59
  174.6 1.5 fusion.99
  178.0 1.5 fusion.105
  181.5 1.5 fusion.111
  183.6 1.3 constant_dynamic-update-slice_fusion.64
  184.9 1.5 fusion.117
  188.4 1.5 fusion.123
  191.8 1.5 fusion.129
  195.2 1.5 fusion.135
  198.7 2.1 fusion.141
  200.9 54.9 %all-gather.10.cloned.1.call-done = f32[16,16,1024]{2,1,0:T(8,128)} async-done(((f32[1,16,1024]{2,1,0:T(8,128)}), f32[16,16,1024]{2,1,0:T(8,128)}) %all-gather.10.cloned.1.call-update) | async-done | bytes 1048592 | tf_op jit(solution)/shard_map/all_gather | solution.py:12
  255.8 12.8 %while.85 = (s32[]{:T(128)}, f32[1,1,1024]{2,1,0:T(1,128)S(1)}, f32[1,16,1024]{2,1,0:T(8,128)S(1)}, s32[]{:T(128)}, f32[16,1,1,1024]{3,2,1,0:T(1,128)S(1)}, /*in...) while((s32[]{:T(128)}, f32[1,1,1024]{2,1,0:T(1,128)S(1)}, f32[1,16,1024]{2,1,0:T(8,128)S(1)}, ...), condition=%wide.region_7.8_spmd, body=%wide.region_6.7_spmd.sunk | while | flops 33797 | bytes 217231 | solution.py:20
  271.2 8.0 %reduce-scatter.13.cloned.1.call-done = f32[1,8,16,128]{3,2,1,0:T(8,128)} async-done(((f32[2,8,16,128]{3,2,1,0:T(8,128)}), f32[1,8,16,128]{3,2,1,0:T(8,128)}) %reduce-scatter.13.cloned.1.call-update) | async-done | bytes 65552 | tf_op jit(solution)/shard_map/reduce_scatter | solution.py:59
  283.3 1.5 constant_dynamic-update-slice_fusion.19
  287.5 1.5 constant_dynamic-update-slice_fusion.18
  290.4 1.3 constant_dynamic-update-slice_fusion.56
  291.7 1.5 constant_dynamic-update-slice_fusion.17
  295.9 1.5 constant_dynamic-update-slice_fusion.16
  300.1 1.5 constant_dynamic-update-slice_fusion.15
  304.3 1.5 constant_dynamic-update-slice_fusion.14
  308.5 1.5 fusion.165
  312.0 8.6 %reduce-scatter.15.cloned.1.call-done = f32[1,8,16,128]{3,2,1,0:T(8,128)} async-done(((f32[2,8,16,128]{3,2,1,0:T(8,128)}), f32[1,8,16,128]{3,2,1,0:T(8,128)}) %reduce-scatter.15.cloned.1.call-update) | async-done | bytes 65552 | tf_op jit(solution)/shard_map/reduce_scatter | solution.py:59
  324.7 1.5 constant_dynamic-update-slice_fusion.26
  328.9 1.5 constant_dynamic-update-slice_fusion.25
  331.8 1.3 constant_dynamic-update-slice_fusion.48
  333.1 1.5 constant_dynamic-update-slice_fusion.24
  337.3 1.5 constant_dynamic-update-slice_fusion.23
  341.5 1.5 constant_dynamic-update-slice_fusion.22
  345.7 1.5 constant_dynamic-update-slice_fusion.21
  349.9 1.5 fusion.159
  353.1 8.8 %reduce-scatter.17.cloned.1.call-done = f32[1,8,16,128]{3,2,1,0:T(8,128)} async-done(((f32[2,8,16,128]{3,2,1,0:T(8,128)}), f32[1,8,16,128]{3,2,1,0:T(8,128)}) %reduce-scatter.17.cloned.1.call-update) | async-done | bytes 65552 | tf_op jit(solution)/shard_map/reduce_scatter | solution.py:59
  363.3 1.5 convert_add_fusion.30
  366.7 1.5 convert_add_fusion.25
  370.1 1.5 convert_add_fusion.20
  372.3 1.3 constant_dynamic-update-slice_fusion.40
  373.6 1.5 convert_add_fusion.15
  377.0 1.5 convert_add_fusion.10
  380.5 1.5 convert_add_fusion.5
  383.9 1.5 convert_add_fusion
  387.3 2.1 bitcast_subtract_fusion
  389.6 54.9 %all-gather.12.cloned.1.call-done = f32[16,16,1024]{2,1,0:T(8,128)} async-done(((f32[1,16,1024]{2,1,0:T(8,128)}), f32[16,16,1024]{2,1,0:T(8,128)}) %all-gather.12.cloned.1.call-update) | async-done | bytes 1048592 | tf_op jit(solution)/shard_map/all_gather | solution.py:12
  444.5 12.8 %while.86 = (s32[]{:T(128)}, f32[1,1,1024]{2,1,0:T(1,128)S(1)}, f32[1,16,1024]{2,1,0:T(8,128)S(1)}, s32[]{:T(128)}, f32[16,1,1,1024]{3,2,1,0:T(1,128)S(1)}, /*in...) while((s32[]{:T(128)}, f32[1,1,1024]{2,1,0:T(1,128)S(1)}, ...), condition=%wide.region_12.13_spmd, body=%wide.region_11.12_spmd.sunk | while | flops 33797 | bytes 217231 | solution.py:20
  (278 shorter events, 155.5 us)
Async XLA Ops:
  7.2 84.1 %copy-start = (bf16[1,1024,1024]{2,1,0:T(8,128)(2,1)S(1)}, bf16[1,1024,1024]{2,1,0:T(8,128)(2,1)}, u32[]{:S(2)}) copy-start(bf16[1,1024,1024]{2,1,0:T(8,128)(2,1)} %param.110) | copy-start | bytes 6291460
  7.2 72.8 %copy-start.1 = (bf16[1,4,128,1024]{3,2,1,0:T(8,128)(2,1)S(1)}, bf16[1,4,128,1024]{3,2,1,0:T(8,128)(2,1)}, u32[]{:S(2)}) copy-start(bf16[1,4,128,1024]{3,2,1,0:T(8,128)(2,1)} %param.113) | copy-start | bytes 3145732
  7.2 73.3 %copy-start.7 = (s32[1,4]{1,0:T(1,128)S(1)}, s32[1,4]{1,0:T(1,128)}, u32[]{:S(2)}) copy-start(s32[1,4]{1,0:T(1,128)} %param.112) | copy-start | bytes 52
  7.2 59.1 %all-gather.8.cloned.1.call-start = ((), (), s32[]{:S(2)}) async-start(), calls=%async_computation.12 | async-start | bytes 1114112 | tf_op jit(solution)/shard_map/all_gather | solution.py:12
  8.4 73.4 %copy-start.2 = (f32[1,1,1024]{2,1,0:T(1,128)S(1)}, f32[1,1,1024]{2,1,0:T(1,128)}, u32[]{:S(2)}) copy-start(f32[1,1,1024]{2,1,0:T(1,128)} %param.111) | copy-start | bytes 12292
  9.1 81.5 %reduce-scatter.7.cloned.1.call-start = ((), (), s32[]{:S(2)}) async-start(), calls=%async_computation.6 | async-start | bytes 196608 | tf_op jit(solution)/shard_map/reduce_scatter | solution.py:59
  81.7 50.2 %reduce-scatter.9.cloned.1.call-start = ((), (), s32[]{:S(2)}) async-start(), calls=%async_computation.7 | async-start | bytes 196608 | tf_op jit(solution)/shard_map/reduce_scatter | solution.py:59
  123.1 50.2 %reduce-scatter.11.cloned.1.call-start = ((), (), s32[]{:S(2)}) async-start(), calls=%async_computation.8 | async-start | bytes 196608 | tf_op jit(solution)/shard_map/reduce_scatter | solution.py:59
  164.4 91.4 %all-gather.10.cloned.1.call-start = ((), (), s32[]{:S(2)}) async-start(), calls=%async_computation.13 | async-start | bytes 1114112 | tf_op jit(solution)/shard_map/all_gather | solution.py:12
  174.0 0.6 copy-start.4
  191.8 6.9 %copy-start.6 = (f32[1,1,1024]{2,1,0:T(1,128)S(1)}, f32[1,1,1024]{2,1,0:T(1,128)}, u32[]{:S(2)}) copy-start(f32[1,1,1024]{2,1,0:T(1,128)} %param.114) | copy-start | bytes 12292
  196.7 71.9 %copy-start.3 = (f32[1,16,1024]{2,1,0:T(8,128)S(1)}, f32[1,16,1024]{2,1,0:T(8,128)}, u32[]{:S(2)}) copy-start(f32[1,16,1024]{2,1,0:T(8,128)} %param.115) | copy-start | bytes 196612
  200.8 78.4 %reduce-scatter.13.cloned.1.call-start = ((), (), s32[]{:S(2)}) async-start(), calls=%async_computation.9 | async-start | bytes 196608 | tf_op jit(solution)/shard_map/reduce_scatter | solution.py:59
  270.4 50.2 %reduce-scatter.15.cloned.1.call-start = ((), (), s32[]{:S(2)}) async-start(), calls=%async_computation.10 | async-start | bytes 196608 | tf_op jit(solution)/shard_map/reduce_scatter | solution.py:59
  311.7 50.2 %reduce-scatter.17.cloned.1.call-start = ((), (), s32[]{:S(2)}) async-start(), calls=%async_computation.11 | async-start | bytes 196608 | tf_op jit(solution)/shard_map/reduce_scatter | solution.py:59
  353.1 91.4 %all-gather.12.cloned.1.call-start = ((), (), s32[]{:S(2)}) async-start(), calls=%async_computation.14 | async-start | bytes 1114112 | tf_op jit(solution)/shard_map/all_gather | solution.py:12
  362.7 0.6 copy-start.5
  389.6 68.4 %copy-start.8 = (bf16[1,8,1,16,1024]{4,3,2,1,0:T(8,128)(2,1)}, bf16[1,8,1,16,1024]{4,3,2,1,0:T(8,128)(2,1)S(1)}, u32[]{:S(2)}) copy-start(bf16[1,8,1,16,1024]{4,3,2,1,0:T(8,128)(2,1)S(1)} %constant_dynamic-update-slice_fusion.28) | copy-start | bytes 786436
Sparse Core Ops, SparseCore 0:
  11.3 54.8 all-gather.7
  81.8 8.7 reduce-scatter.6
  123.2 8.7 reduce-scatter.8
  164.5 8.7 reduce-scatter.10
  200.9 54.8 all-gather.9
  270.5 8.7 reduce-scatter.12
  311.9 8.7 reduce-scatter.14
  353.2 8.7 reduce-scatter.16
  389.6 54.8 all-gather.11
where the time goes:
time: 473 us; the launch traced here: 464 us
  waiting for transfers between devices  183 us (39%)
  other arithmetic  123 us (26%)
  matrix products  75.2 us (16%)
  blocking collectives  35 us (7%)
  local copies, waits for them, and re-layouts  32.1 us (7%)
  between operations  14.3 us (3%)
    all_gather x3, waiting for transfers between devices, carried_in(): gathered = jax.tree.map(lambda a: lax.all_gather(a, axis), part)  132 us
    dot_general x48, matrix products, shards(): jnp.einsum('smn,sqn->sqm', block_inverse, drive_term.astype(jnp.bfloat16)...  69.2 us
    scatter-add x48, other arithmetic, shards(): drive_term = drive_term.at[:, :, :port_count].add(inflow[:, step_index])  58.8 us
    reduce_scatter x6, waiting for transfers between devices, shards(): lax.psum_scatter(jnp.einsum('skg,sktqp->gtqp', owners, jnp.einsum('skpn,t...  50.9 us
    add x42, other arithmetic, compose(): return (earlier[0] * latter[0], latter[0] * earlier[1] + latter[1])  36.7 us
    all_gather x1, blocking collectives, carried_in(): gathered = jax.tree.map(lambda a: lax.all_gather(a, axis), part)  35 us
    unnamed x71, local copies, waits for them, and re-layouts  28.1 us
    add x30, other arithmetic, shards(): drive_term = factor * previous + own_sources[step_index].astype(jnp.float32)  23.5 us
  transfers between devices with their start and end apart: 9, of which 9 were waited for; matrix products, arithmetic and copies ran while one was open for 0% of the time, Pallas kernels for 0%

commit v1 on v0

v1 whole, which is shorter than its diff:
```python
import functools

import jax
import jax.numpy as jnp
from jax import lax
from jax.experimental import pallas as pl
from jax.experimental.pallas import tpu as pltpu
from jax.sharding import PartitionSpec as P

SWEEPS = 3
ITERS = 2
MESH = pl.DeviceIdType.MESH
F32 = jnp.float32
BF16 = jnp.bfloat16
SUB, LANE = 8, 128


def dot(a, b):
    return jnp.dot(a.astype(BF16), b.astype(BF16), preferred_element_type=F32)


def kernel(
    cuts,
    circ,
    steps,
    src_ref,
    inv_ref,
    mem_ref,
    tgt_ref,
    cw_ref,
    dec_ref,
    init_ref,
    start_ref,
    wave_ref,
    inv_t,
    pow1,
    pow2,
    pow4,
    port_t,
    resp,
    port_resp,
    own,
    free,
    terms_buf,
    gather_buf,
    chain_buf,
    state_buf,
    decay_buf,
    part_buf,
    inflow_buf,
    send1,
    recv1,
    send2,
    recv2,
    send_d,
    recv_d,
    send_x,
    recv_x,
):
    n = lax.axis_index("cuts")
    me = lax.axis_index("circ")
    nodes = inv_ref.shape[0]
    scen = init_ref.shape[0]
    rows = src_ref.shape[0]
    blocks, ports = cw_ref.shape[0], cw_ref.shape[1]
    cols = nodes // LANE
    pieces = (scen // SUB) * cols
    stride = cuts // pieces
    piece = n // stride
    owner = lax.rem(n, stride) == 0

    def cut(k):
        return lax.rem(n + k, cuts)

    def peer(k):
        return lax.rem(me + k, circ)

    barrier = pltpu.get_barrier_semaphore()

    @pl.loop(1, cuts)
    def _(k):
        pl.semaphore_signal(barrier, inc=1, device_id=(cut(k), me), device_id_type=MESH)

    for k in range(1, circ):
        pl.semaphore_signal(barrier, inc=1, device_id=(n, peer(k)), device_id_type=MESH)

    def tile(p):
        r, c = p // cols, p % cols
        return slice(r * SUB, (r + 1) * SUB), slice(c * LANE, (c + 1) * LANE)

    def term_copy(c, other, dest, source):
        return pltpu.make_async_remote_copy(
            src_ref=terms_buf.at[c, dest // stride],
            dst_ref=gather_buf.at[c, source],
            send_sem=send1.at[c, dest // stride],
            recv_sem=recv1.at[c, source],
            device_id=(other, me),
            device_id_type=MESH,
        )

    def decay_copy(other, dest, source):
        lane = pl.multiple_of(lax.rem(dest // stride, cols) * LANE, LANE)
        return pltpu.make_async_remote_copy(
            src_ref=dec_ref.at[:, pl.ds(lane, LANE)],
            dst_ref=decay_buf.at[source],
            send_sem=send_d.at[dest // stride],
            recv_sem=recv_d.at[source],
            device_id=(other, me),
            device_id_type=MESH,
        )

    def state_copy(c, other, dest, source_piece):
        return pltpu.make_async_remote_copy(
            src_ref=chain_buf.at[c, dest],
            dst_ref=state_buf.at[c, source_piece],
            send_sem=send2.at[c, dest],
            recv_sem=recv2.at[c, source_piece],
            device_id=(other, me),
            device_id_type=MESH,
        )

    def is_owner(d):
        return lax.rem(d, stride) == 0

    def chain_send(c, terms):
        for p in range(pieces):
            terms_buf[c, p] = terms[tile(p)]
        if c == 0:
            pl.semaphore_wait(barrier, cuts - 1 + circ - 1)

        @pl.loop(1, cuts)
        def _(k):
            d = cut(k)

            @pl.when(is_owner(d))
            def _():
                term_copy(c, d, d, n).start()
                if c == 0:
                    decay_copy(d, d, n).start()

    def chain_turn(c):
        @pl.when(owner)
        def _():
            if c == 0:
                lane = pl.multiple_of(lax.rem(piece, cols) * LANE, LANE)
                decay_buf[n] = dec_ref[:, pl.ds(lane, LANE)]
            gather_buf[c, n] = terms_buf[c, piece]

            @pl.loop(1, cuts)
            def _(k):
                s = cut(k)
                term_copy(c, s, n, s).wait_recv()
                if c == 0:
                    decay_copy(s, n, s).wait_recv()

            row = pl.multiple_of(piece // cols * SUB, SUB)
            lane = pl.multiple_of(lax.rem(piece, cols) * LANE, LANE)
            state = init_ref[pl.ds(row, SUB), pl.ds(lane, LANE)]
            for s in range(cuts):
                chain_buf[c, s] = state
                if s < cuts - 1:
                    state = decay_buf[s] * state + gather_buf[c, s]

            @pl.loop(1, cuts)
            def _(k):
                d = cut(k)
                state_copy(c, d, d, piece).start()

            state_buf[c, piece] = chain_buf[c, n]

    def chain_end(c):
        @pl.loop(1, cuts)
        def _(k):
            s = cut(k)

            @pl.when(is_owner(s))
            def _():
                state_copy(c, s, n, s // stride).wait_recv()

        return jnp.concatenate(
            [
                jnp.concatenate([state_buf[c, r * cols + q] for q in range(cols)], axis=1)
                for r in range(scen // SUB)
            ],
            axis=0,
        )

    def drain(c):
        @pl.loop(1, cuts)
        def _(k):
            d = cut(k)

            @pl.when(is_owner(d))
            def _():
                term_copy(c, d, d, n).wait_send()
                if c == 0:
                    decay_copy(d, d, n).wait_send()

            @pl.when(owner)
            def _():
                state_copy(c, d, d, piece).wait_send()

    def current_copy(e, height, k, source):
        return pltpu.make_async_remote_copy(
            src_ref=part_buf.at[e, peer(k), pl.ds(0, height)],
            dst_ref=inflow_buf.at[e, source, pl.ds(0, height)],
            send_sem=send_x.at[e, k - 1],
            recv_sem=recv_x.at[e, source],
            device_id=(n, peer(k)),
            device_id_type=MESH,
        )

    def exchange_start(e, partial):
        height = partial.shape[0]
        for g in range(circ):
            part_buf[e, g, 0:height] = partial[:, g * ports : (g + 1) * ports]
        for k in range(1, circ):
            current_copy(e, height, k, me).start()

    def exchange_end(e, height):
        total = part_buf[e, me, 0:height]
        for k in range(1, circ):
            current_copy(e, height, k, peer(k)).wait_recv()
            total = total + inflow_buf[e, peer(k), 0:height]
        return total

    def exchange_drain(e, height):
        for k in range(1, circ):
            current_copy(e, height, k, me).wait_send()

    wide = min(256, nodes)

    def product(out, left, right):
        @pl.loop(0, nodes, step=wide)
        def _(at):
            at = pl.multiple_of(at, wide)
            out[:, pl.ds(at, wide)] = dot(left[...], right[:, pl.ds(at, wide)]).astype(BF16)

    load = src_ref[0:scen].astype(F32)
    for t in range(1, steps):
        load = load + src_ref[t * scen : (t + 1) * scen].astype(F32)
    chain_send(0, load * (1.0 / steps))

    factor = jnp.broadcast_to(mem_ref[...], (LANE, nodes)).T
    for c in range(cols):
        at = slice(c * LANE, (c + 1) * LANE)
        turned = inv_ref[at, :].T
        inv_t[:, at] = turned
        pow1[:, at] = (turned.astype(F32) * factor).astype(BF16)
    product(pow2, pow1, pow1)
    own[...] = dot(src_ref[...], inv_t[...])
    own[scen:] = own[scen:] + dot(own[: rows - scen], pow1[...])

    chain_turn(0)

    product(pow4, pow2, pow2)
    span = 2
    for power in (pow2, pow4):
        if span < steps:
            own[span * scen :] = own[span * scen :] + dot(own[: rows - span * scen], power[...])
        span *= 2
    resp[0:ports] = inv_t[0:ports]
    resp[ports : 2 * ports] = dot(resp[0:ports], pow1[...]).astype(BF16)
    resp[2 * ports : 4 * ports] = dot(resp[0 : 2 * ports], pow2[...]).astype(BF16)
    resp[4 * ports : 8 * ports] = dot(resp[0 : 4 * ports], pow4[...]).astype(BF16)
    for g in range(circ):
        summed = jnp.zeros((ports, nodes), F32)
        for b in range(blocks):
            share = jnp.where(tgt_ref[0, b] == g, 1.0, 0.0).astype(F32)
            summed = summed + share * cw_ref[b].astype(F32)
        port_t[:, g * ports : (g + 1) * ports] = summed.astype(BF16).T
    port_resp[...] = dot(resp[...], port_t[...]).astype(BF16)

    def by_lag(currents):
        low = currents.astype(BF16)
        columns = [low]
        for lag in range(1, steps):
            columns.append(
                jnp.concatenate(
                    [jnp.zeros((lag * scen, ports), BF16), low[: rows - lag * scen]], axis=0
                )
            )
        return jnp.concatenate(columns, axis=1)

    begin = chain_end(0)
    last = rows - scen
    for iteration in range(ITERS):
        first = iteration * SWEEPS
        exchange_start(first, dot(begin, port_t[...]))
        v0 = begin.astype(BF16)
        v1 = dot(v0, pow1[...])
        v01 = jnp.concatenate([v0, v1.astype(BF16)], axis=0)
        v23 = dot(v01, pow2[...])
        v03 = jnp.concatenate([v01, v23.astype(BF16)], axis=0)
        v47 = dot(v03, pow4[...])
        v8 = dot(v47[0:scen], pow4[...])
        free[0:scen] = own[0:scen] + v1
        free[scen : 3 * scen] = own[scen : 3 * scen] + v23
        free[3 * scen : last] = own[3 * scen : last] + v47
        free[last:] = own[last:] + v8
        seen = dot(free[...], port_t[...])
        current = exchange_end(first, scen)
        current = jnp.concatenate([current] * steps, axis=0)
        for sweep in range(1, SWEEPS):
            exchange_start(first + sweep, seen + dot(by_lag(current), port_resp[...]))
            current = exchange_end(first + sweep, rows)
        lags = by_lag(current)
        if iteration < ITERS - 1:
            final = free[last:] + dot(lags[last:], resp[...])
        else:
            wave = free[...] + dot(lags, resp[...])
            wave_ref[...] = wave.astype(BF16)
            final = wave[last:]
        chain_send(iteration + 1, final - dec_ref[...] * begin)
        chain_turn(iteration + 1)
        begin = chain_end(iteration + 1)
    start_ref[...] = begin

    for c in range(ITERS + 1):
        drain(c)
    for e in range(SWEEPS * ITERS):
        exchange_drain(e, scen if e % SWEEPS == 0 else rows)


def solution(mesh):
    cuts, circ = mesh.shape["cuts"], mesh.shape["circ"]

    def shards(sources, inverse, memory, target, weight, decay, initial):
        steps, scen, nodes = sources.shape[1], sources.shape[3], sources.shape[4]
        blocks, ports = weight.shape[1], weight.shape[2]
        rows = steps * scen
        pieces = scen * nodes // (SUB * LANE)
        chains, swaps = ITERS + 1, ITERS * SWEEPS
        vmem = pl.BlockSpec(memory_space=pltpu.VMEM)
        smem = pl.BlockSpec(memory_space=pltpu.SMEM)
        dma = pltpu.SemaphoreType.DMA
        square = pltpu.VMEM((nodes, nodes), BF16)
        start, wave = pl.pallas_call(
            functools.partial(kernel, cuts, circ, steps),
            out_shape=(
                jax.ShapeDtypeStruct((scen, nodes), F32),
                jax.ShapeDtypeStruct((rows, nodes), BF16),
            ),
            in_specs=[vmem, vmem, vmem, smem, vmem, vmem, vmem],
            out_specs=(vmem, vmem),
            scratch_shapes=[
                square,
                square,
                square,
                square,
                pltpu.VMEM((nodes, circ * ports), BF16),
                pltpu.VMEM((steps * ports, nodes), BF16),
                pltpu.VMEM((steps * ports, circ * ports), BF16),
                pltpu.VMEM((rows, nodes), F32),
                pltpu.VMEM((rows, nodes), F32),
                pltpu.VMEM((chains, pieces, SUB, LANE), F32),
                pltpu.VMEM((chains, cuts, SUB, LANE), F32),
                pltpu.VMEM((chains, cuts, SUB, LANE), F32),
                pltpu.VMEM((chains, pieces, SUB, LANE), F32),
                pltpu.VMEM((cuts, 1, LANE), F32),
                pltpu.VMEM((swaps, circ, rows, ports), F32),
                pltpu.VMEM((swaps, circ, rows, ports), F32),
                dma((chains, pieces)),
                dma((chains, cuts)),
                dma((chains, cuts)),
                dma((chains, pieces)),
                dma((pieces,)),
                dma((cuts,)),
                dma((swaps, max(circ - 1, 1))),
                dma((swaps, circ)),
            ],
            compiler_params=pltpu.CompilerParams(
                collective_id=0, has_side_effects=True, vmem_limit_bytes=60 * 1024 * 1024
            ),
            name="parareal",
        )(
            sources.reshape(rows, nodes),
            inverse[0],
            memory.reshape(1, nodes),
            target,
            weight[0],
            decay.reshape(1, nodes),
            initial[0],
        )
        return start[None, None], wave.reshape(1, steps, 1, scen, nodes)

    return jax.shard_map(
        shards,
        mesh=mesh,
        in_specs=(
            P("cuts", None, "circ", None, None),
            P("circ", None, None),
            P("cuts", "circ", None),
            P("circ", None),
            P("circ", None, None, None),
            P("cuts", "circ", None),
            P("circ", None, None),
        ),
        out_specs=(P("cuts", "circ", None, None), P("cuts", None, "circ", None, None)),
        check_vma=False,
    )
```

time: 473 us -> 57.2 us (0.12)
  the two profiles are of different devices: /device:TPU:28 before, /device:TPU:0 now
where the time goes in v1:
time: 57.2 us; the launch traced here: 57 us
  Pallas kernels  53.2 us (93%)
  local copies, waits for them, and re-layouts  3.14 us (5%)
  between operations  0.64 us (1%)
    pallas_call x1, Pallas kernels, shards(): pl.pallas_call(functools.partial(kernel, cuts, circ, steps), out_shape=(j...  53.2 us
    unnamed x2, local copies, waits for them, and re-layouts  3.14 us

profile of v1, /device:TPU:0, one launch (start us, length us, event | category | flops | bytes accessed | tf_op | source)
XLA Modules:
  0.0 57.0 jit_solution(16692125074568049319)
XLA Ops:
  0.6 53.2 %parareal.1 = (f32[16,1024]{1,0:T(8,128)}, bf16[128,1024]{1,0:T(8,128)(2,1)}) custom-call(bf16[128,1024]{1,0:T(8,128)(2,1)} %bitcast.12, bf16[1024,1024]{1,0:T(8,128)(2,1)} %bitcast.10, f32[1,1024]{1,0:T(1,128)} %bitcast.16, s32[1,4]{1,0:T(1,128)} %tgt_ref.1, bf16[4,128,1024]{2,1,0:T(8,128)(2,1)} %bitcast.11, f32[1,1024]{1,0:T(1,128)} %bitcast.17, ...), custom_call_target="tpu_custom_call" | custom-call | tf_op jit(solution)/shard_map/parareal/pallas_call | solution.py:338
  53.9 1.5 %copy.12 = f32[1,1,16,1024]{3,2,1,0:T(8,128)} copy(f32[1,1,16,1024]{3,2,1,0:T(8,128)} %bitcast.15) | data formatting | bytes 131072
  55.3 1.7 %copy.13 = bf16[1,8,1,16,1024]{4,3,2,1,0:T(8,128)(2,1)} copy(bf16[1,8,1,16,1024]{4,3,2,1,0:T(8,128)(2,1)} %bitcast.13) | data formatting | bytes 524288

commit v2 on v1

--- a/solution.py
+++ b/solution.py
@@ -12,7 +12,7 @@
 MESH = pl.DeviceIdType.MESH
 F32 = jnp.float32
 BF16 = jnp.bfloat16
-SUB, LANE = 8, 128
+LANE = 128
 
 
 def dot(a, b):
@@ -23,6 +23,15 @@
     cuts,
     circ,
     steps,
+    src_in,
+    inv_in,
+    mem_in,
+    tgt_in,
+    cw_in,
+    dec_in,
+    init_in,
+    start_ref,
+    wave_out,
     src_ref,
     inv_ref,
     mem_ref,
@@ -30,8 +39,9 @@
     cw_ref,
     dec_ref,
     init_ref,
-    start_ref,
     wave_ref,
+    sem_in,
+    sem_out,
     inv_t,
     pow1,
     pow2,
@@ -64,10 +74,10 @@
     rows = src_ref.shape[0]
     blocks, ports = cw_ref.shape[0], cw_ref.shape[1]
     cols = nodes // LANE
-    pieces = (scen // SUB) * cols
-    stride = cuts // pieces
-    piece = n // stride
-    owner = lax.rem(n, stride) == 0
+    base = (cuts - cols) // 2
+    piece = n - base
+    owner = jnp.logical_and(n >= base, n < base + cols)
+    lane = pl.multiple_of(piece * LANE, LANE)
 
     def cut(k):
         return lax.rem(n + k, cuts)
@@ -84,120 +94,108 @@
     for k in range(1, circ):
         pl.semaphore_signal(barrier, inc=1, device_id=(n, peer(k)), device_id_type=MESH)
 
-    def tile(p):
-        r, c = p // cols, p % cols
-        return slice(r * SUB, (r + 1) * SUB), slice(c * LANE, (c + 1) * LANE)
-
-    def term_copy(c, other, dest, source):
+    pairs = (
+        (dec_in, dec_ref),
+        (src_in, src_ref),
+        (inv_in, inv_ref),
+        (mem_in, mem_ref),
+        (cw_in, cw_ref),
+        (tgt_in, tgt_ref),
+        (init_in, init_ref),
+    )
+    loads = [pltpu.make_async_copy(a, b, sem_in.at[k]) for k, (a, b) in enumerate(pairs)]
+    for copy in loads:
+        copy.start()
+
+    def term_copy(c, k, dest, source):
         return pltpu.make_async_remote_copy(
-            src_ref=terms_buf.at[c, dest // stride],
+            src_ref=terms_buf.at[c, k],
             dst_ref=gather_buf.at[c, source],
-            send_sem=send1.at[c, dest // stride],
+            send_sem=send1.at[c, k],
             recv_sem=recv1.at[c, source],
+            device_id=(dest, me),
+            device_id_type=MESH,
+        )
+
+    def decay_copy(k, dest, source):
+        return pltpu.make_async_remote_copy(
+            src_ref=dec_ref.at[:, pl.ds(k * LANE, LANE)],
+            dst_ref=decay_buf.at[source],
+            send_sem=send_d.at[k],
+            recv_sem=recv_d.at[source],
+            device_id=(dest, me),
+            device_id_type=MESH,
+        )
+
+    def state_copy(c, dest, other, k):
+        return pltpu.make_async_remote_copy(
+            src_ref=chain_buf.at[c, dest],
+            dst_ref=state_buf.at[c, k],
+            send_sem=send2.at[c, dest],
+            recv_sem=recv2.at[c, k],
             device_id=(other, me),
             device_id_type=MESH,
         )
 
-    def decay_copy(other, dest, source):
-        lane = pl.multiple_of(lax.rem(dest // stride, cols) * LANE, LANE)
-        return pltpu.make_async_remote_copy(
-            src_ref=dec_ref.at[:, pl.ds(lane, LANE)],
-            dst_ref=decay_buf.at[source],
-            send_sem=send_d.at[dest // stride],
-            recv_sem=recv_d.at[source],
-            device_id=(other, me),
-            device_id_type=MESH,
-        )
-
-    def state_copy(c, other, dest, source_piece):
-        return pltpu.make_async_remote_copy(
-            src_ref=chain_buf.at[c, dest],
-            dst_ref=state_buf.at[c, source_piece],
-            send_sem=send2.at[c, dest],
-            recv_sem=recv2.at[c, source_piece],
-            device_id=(other, me),
-            device_id_type=MESH,
-        )
-
-    def is_owner(d):
-        return lax.rem(d, stride) == 0
+    def sends_to(dest):
+        return jnp.logical_and(n != dest, n < cuts - 1)
 
     def chain_send(c, terms):
-        for p in range(pieces):
-            terms_buf[c, p] = terms[tile(p)]
-        if c == 0:
-            pl.semaphore_wait(barrier, cuts - 1 + circ - 1)
-
-        @pl.loop(1, cuts)
-        def _(k):
-            d = cut(k)
-
-            @pl.when(is_owner(d))
+        for k in range(cols):
+            terms_buf[c, k] = terms[:, k * LANE : (k + 1) * LANE]
+        for k in range(cols):
+
+            @pl.when(sends_to(base + k))
             def _():
-                term_copy(c, d, d, n).start()
+                term_copy(c, k, base + k, n).start()
                 if c == 0:
-                    decay_copy(d, d, n).start()
+                    decay_copy(k, base + k, n).start()
 
     def chain_turn(c):
         @pl.when(owner)
         def _():
             if c == 0:
-                lane = pl.multiple_of(lax.rem(piece, cols) * LANE, LANE)
                 decay_buf[n] = dec_ref[:, pl.ds(lane, LANE)]
             gather_buf[c, n] = terms_buf[c, piece]
-
-            @pl.loop(1, cuts)
-            def _(k):
-                s = cut(k)
-                term_copy(c, s, n, s).wait_recv()
-                if c == 0:
-                    decay_copy(s, n, s).wait_recv()
-
-            row = pl.multiple_of(piece // cols * SUB, SUB)
-            lane = pl.multiple_of(lax.rem(piece, cols) * LANE, LANE)
-            state = init_ref[pl.ds(row, SUB), pl.ds(lane, LANE)]
+            state = init_ref[:, pl.ds(lane, LANE)]
             for s in range(cuts):
                 chain_buf[c, s] = state
+
+                @pl.when(n != s)
+                def _():
+                    state_copy(c, s, s, piece).start()
+                    if s < cuts - 1:
+                        term_copy(c, 0, s, s).wait_recv()
+                        if c == 0:
+                            decay_copy(0, s, s).wait_recv()
+
                 if s < cuts - 1:
                     state = decay_buf[s] * state + gather_buf[c, s]
-
+            state_buf[c, piece] = chain_buf[c, n]
+
+    def chain_end(c):
+        for k in range(cols):
+
+            @pl.when(n != base + k)
+            def _():
+                state_copy(c, 0, base + k, k).wait_recv()
+
+        return jnp.concatenate([state_buf[c, k] for k in range(cols)], axis=1)
+
+    def drain(c):
+        for k in range(cols):
+
+            @pl.when(sends_to(base + k))
+            def _():
+                term_copy(c, k, base + k, n).wait_send()
+                if c == 0:
+                    decay_copy(k, base + k, n).wait_send()
+
+        @pl.when(owner)
+        def _():
             @pl.loop(1, cuts)
             def _(k):
                 d = cut(k)
-                state_copy(c, d, d, piece).start()
-
-            state_buf[c, piece] = chain_buf[c, n]
-
-    def chain_end(c):
-        @pl.loop(1, cuts)
-        def _(k):
-            s = cut(k)
-
-            @pl.when(is_owner(s))
-            def _():
-                state_copy(c, s, n, s // stride).wait_recv()
-
-        return jnp.concatenate(
-            [
-                jnp.concatenate([state_buf[c, r * cols + q] for q in range(cols)], axis=1)
-                for r in range(scen // SUB)
-            ],
-            axis=0,
-        )
-
-    def drain(c):
-        @pl.loop(1, cuts)
-        def _(k):
-            d = cut(k)
-
-            @pl.when(is_owner(d))
-            def _():
-                term_copy(c, d, d, n).wait_send()
-                if c == 0:
-                    decay_copy(d, d, n).wait_send()
-
-            @pl.when(owner)
-            def _():
                 state_copy(c, d, d, piece).wait_send()
 
     def current_copy(e, height, k, source):
@@ -236,23 +234,42 @@
             at = pl.multiple_of(at, wide)
             out[:, pl.ds(at, wide)] = dot(left[...], right[:, pl.ds(at, wide)]).astype(BF16)
 
-    load = src_ref[0:scen].astype(F32)
-    for t in range(1, steps):
-        load = load + src_ref[t * scen : (t + 1) * scen].astype(F32)
-    chain_send(0, load * (1.0 / steps))
-
+    for copy in loads[:4]:
+        copy.wait()
     factor = jnp.broadcast_to(mem_ref[...], (LANE, nodes)).T
     for c in range(cols):
         at = slice(c * LANE, (c + 1) * LANE)
         turned = inv_ref[at, :].T
         inv_t[:, at] = turned
         pow1[:, at] = (turned.astype(F32) * factor).astype(BF16)
+    for copy in loads[4:]:
+        copy.wait()
+    for g in range(circ):
+        summed = jnp.zeros((ports, nodes), F32)
+        for b in range(blocks):
+            share = jnp.where(tgt_ref[0, b] == g, 1.0, 0.0).astype(F32)
+            summed = summed + share * cw_ref[b].astype(F32)
+        port_t[:, g * ports : (g + 1) * ports] = summed.astype(BF16).T
+
+    load = src_ref[0:scen].astype(F32)
+    for t in range(1, steps):
+        load = load + src_ref[t * scen : (t + 1) * scen].astype(F32)
+    pl.semaphore_wait(barrier, cuts - 1 + circ - 1)
+    chain_send(0, load * (1.0 / steps))
+
+    def one_step(values):
+        exact = mem_ref[...] * values
+        high = exact.astype(BF16)
+        low = (exact - high.astype(F32)).astype(BF16)
+        both = dot(jnp.concatenate([high, low], axis=0), inv_t[...])
+        return both[: values.shape[0]] + both[values.shape[0] :]
+
     product(pow2, pow1, pow1)
     own[...] = dot(src_ref[...], inv_t[...])
-    own[scen:] = own[scen:] + dot(own[: rows - scen], pow1[...])
 
     chain_turn(0)
 
+    own[scen:] = own[scen:] + one_step(own[: rows - scen])
     product(pow4, pow2, pow2)
     span = 2
     for power in (pow2, pow4):
@@ -263,12 +280,6 @@
     resp[ports : 2 * ports] = dot(resp[0:ports], pow1[...]).astype(BF16)
     resp[2 * ports : 4 * ports] = dot(resp[0 : 2 * ports], pow2[...]).astype(BF16)
     resp[4 * ports : 8 * ports] = dot(resp[0 : 4 * ports], pow4[...]).astype(BF16)
-    for g in range(circ):
-        summed = jnp.zeros((ports, nodes), F32)
-        for b in range(blocks):
-            share = jnp.where(tgt_ref[0, b] == g, 1.0, 0.0).astype(F32)
-            summed = summed + share * cw_ref[b].astype(F32)
-        port_t[:, g * ports : (g + 1) * ports] = summed.astype(BF16).T
     port_resp[...] = dot(resp[...], port_t[...]).astype(BF16)
 
     def by_lag(currents):
@@ -288,7 +299,7 @@
         first = iteration * SWEEPS
         exchange_start(first, dot(begin, port_t[...]))
         v0 = begin.astype(BF16)
-        v1 = dot(v0, pow1[...])
+        v1 = one_step(begin)
         v01 = jnp.concatenate([v0, v1.astype(BF16)], axis=0)
         v23 = dot(v01, pow2[...])
         v03 = jnp.concatenate([v01, v23.astype(BF16)], axis=0)
@@ -310,11 +321,14 @@
         else:
             wave = free[...] + dot(lags, resp[...])
             wave_ref[...] = wave.astype(BF16)
+            result = pltpu.make_async_copy(wave_ref, wave_out, sem_out)
+            result.start()
             final = wave[last:]
         chain_send(iteration + 1, final - dec_ref[...] * begin)
         chain_turn(iteration + 1)
         begin = chain_end(iteration + 1)
     start_ref[...] = begin
+    result.wait()
 
     for c in range(ITERS + 1):
         drain(c)
@@ -329,10 +343,10 @@
         steps, scen, nodes = sources.shape[1], sources.shape[3], sources.shape[4]
         blocks, ports = weight.shape[1], weight.shape[2]
         rows = steps * scen
-        pieces = scen * nodes // (SUB * LANE)
+        cols = nodes // LANE
         chains, swaps = ITERS + 1, ITERS * SWEEPS
         vmem = pl.BlockSpec(memory_space=pltpu.VMEM)
-        smem = pl.BlockSpec(memory_space=pltpu.SMEM)
+        hbm = pl.BlockSpec(memory_space=pl.ANY)
         dma = pltpu.SemaphoreType.DMA
         square = pltpu.VMEM((nodes, nodes), BF16)
         start, wave = pl.pallas_call(
@@ -341,9 +355,19 @@
                 jax.ShapeDtypeStruct((scen, nodes), F32),
                 jax.ShapeDtypeStruct((rows, nodes), BF16),
             ),
-            in_specs=[vmem, vmem, vmem, smem, vmem, vmem, vmem],
-            out_specs=(vmem, vmem),
+            in_specs=[hbm] * 7,
+            out_specs=(vmem, hbm),
             scratch_shapes=[
+                pltpu.VMEM((rows, nodes), BF16),
+                square,
+                pltpu.VMEM((1, nodes), F32),
+                pltpu.SMEM((1, blocks), jnp.int32),
+                pltpu.VMEM((blocks, ports, nodes), BF16),
+                pltpu.VMEM((1, nodes), F32),
+                pltpu.VMEM((scen, nodes), F32),
+                pltpu.VMEM((rows, nodes), BF16),
+                dma((7,)),
+                dma(()),
                 square,
                 square,
                 square,
@@ -353,18 +377,18 @@
                 pltpu.VMEM((steps * ports, circ * ports), BF16),
                 pltpu.VMEM((rows, nodes), F32),
                 pltpu.VMEM((rows, nodes), F32),
-                pltpu.VMEM((chains, pieces, SUB, LANE), F32),
-                pltpu.VMEM((chains, cuts, SUB, LANE), F32),
-                pltpu.VMEM((chains, cuts, SUB, LANE), F32),
-                pltpu.VMEM((chains, pieces, SUB, LANE), F32),
+                pltpu.VMEM((chains, cols, scen, LANE), F32),
+                pltpu.VMEM((chains, cuts, scen, LANE), F32),
+                pltpu.VMEM((chains, cuts, scen, LANE), F32),
+                pltpu.VMEM((chains, cols, scen, LANE), F32),
                 pltpu.VMEM((cuts, 1, LANE), F32),
                 pltpu.VMEM((swaps, circ, rows, ports), F32),
                 pltpu.VMEM((swaps, circ, rows, ports), F32),
-                dma((chains, pieces)),
+                dma((chains, cols)),
                 dma((chains, cuts)),
                 dma((chains, cuts)),
-                dma((chains, pieces)),
-                dma((pieces,)),
+                dma((chains, cols)),
+                dma((cols,)),
                 dma((cuts,)),
                 dma((swaps, max(circ - 1, 1))),
                 dma((swaps, circ)),

time: 57.2 us -> 48.7 us (0.85)
  the two profiles are of different devices: /device:TPU:0 before, /device:TPU:8 now
where the time goes in v2:
time: 48.7 us; the launch traced here: 48.5 us
  Pallas kernels  44.7 us (92%)
  local copies, waits for them, and re-layouts  3.14 us (6%)
  between operations  0.64 us (1%)
    pallas_call x1, Pallas kernels, shards(): pl.pallas_call(functools.partial(kernel, cuts, circ, steps), out_shape=(j...  44.7 us
    unnamed x2, local copies, waits for them, and re-layouts  3.14 us

profile of v2, /device:TPU:8, one launch (start us, length us, event | category | flops | bytes accessed | tf_op | source)
XLA Modules:
  0.0 48.5 jit_solution(11273173036932801386)
XLA Ops:
  0.6 44.7 %parareal.1 = (f32[16,1024]{1,0:T(8,128)}, bf16[128,1024]{1,0:T(8,128)(2,1)}) custom-call(bf16[128,1024]{1,0:T(8,128)(2,1)} %bitcast.12, bf16[1024,1024]{1,0:T(8,128)(2,1)} %bitcast.10, f32[1,1024]{1,0:T(1,128)} %bitcast.16, s32[1,4]{1,0:T(1,128)} %tgt_in.1, bf16[4,128,1024]{2,1,0:T(8,128)(2,1)} %bitcast.11, f32[1,1024]{1,0:T(1,128)} %bitcast.17, ...), custom_call_target="tpu_custom_call" | custom-call | tf_op jit(solution)/shard_map/parareal/pallas_call | solution.py:352
  45.3 1.5 %copy.12 = f32[1,1,16,1024]{3,2,1,0:T(8,128)} copy(f32[1,1,16,1024]{3,2,1,0:T(8,128)} %bitcast.15) | data formatting | bytes 131072
  46.8 1.7 %copy.13 = bf16[1,8,1,16,1024]{4,3,2,1,0:T(8,128)(2,1)} copy(bf16[1,8,1,16,1024]{4,3,2,1,0:T(8,128)(2,1)} %bitcast.13) | data formatting | bytes 524288

commit v3 on v2

--- a/solution.py
+++ b/solution.py
@@ -334,6 +334,11 @@
         drain(c)
     for e in range(SWEEPS * ITERS):
         exchange_drain(e, scen if e % SWEEPS == 0 else rows)
+
+
+def hand_over(start_in, wave_in, start_out, wave_out):
+    start_out[...] = start_in[...]
+    wave_out[...] = wave_in[...]
 
 
 def solution(mesh):
@@ -406,6 +411,16 @@
             decay.reshape(1, nodes),
             initial[0],
         )
+        start, wave = pl.pallas_call(
+            hand_over,
+            out_shape=(
+                jax.ShapeDtypeStruct(start.shape, F32),
+                jax.ShapeDtypeStruct(wave.shape, BF16),
+            ),
+            in_specs=[vmem, vmem],
+            out_specs=(vmem, vmem),
+            name="hand_over",
+        )(start, wave)
         return start[None, None], wave.reshape(1, steps, 1, scen, nodes)
 
     return jax.shard_map(

time: 48.7 us -> 47.3 us (0.971)
  local copies, waits for them, and re-layouts: 3.14 us -> 0 us
  Pallas kernels: 44.7 us -> 46.4 us
    unnamed x2 -> x0, local copies, waits for them, and re-layouts: 3.14 us -> none
    pallas_call x0 -> x1, Pallas kernels: none -> 1.72 us  [shards(): pl.pallas_call(hand_over, out_shape=(jax.ShapeDtypeStruct(start.shape, F3...]
where the time goes in v3:
time: 47.3 us; the launch traced here: 47.1 us
  Pallas kernels  46.4 us (98%)
  between operations  0.64 us (1%)
    pallas_call x1, Pallas kernels, shards(): pl.pallas_call(functools.partial(kernel, cuts, circ, steps), out_shape=(j...  44.7 us
    pallas_call x1, Pallas kernels, shards(): pl.pallas_call(hand_over, out_shape=(jax.ShapeDtypeStruct(start.shape, F3...  1.72 us

profile of v3, /device:TPU:8, one launch (start us, length us, event | category | flops | bytes accessed | tf_op | source)
XLA Modules:
  0.0 47.1 jit_solution(8651123869191276798)
XLA Ops:
  0.6 44.7 %parareal.1 = (f32[16,1024]{1,0:T(8,128)}, bf16[128,1024]{1,0:T(8,128)(2,1)}) custom-call(bf16[128,1024]{1,0:T(8,128)(2,1)} %bitcast.12, bf16[1024,1024]{1,0:T(8,128)(2,1)} %bitcast.10, f32[1,1024]{1,0:T(1,128)} %bitcast.14, s32[1,4]{1,0:T(1,128)} %tgt_in.1, bf16[4,128,1024]{2,1,0:T(8,128)(2,1)} %bitcast.11, f32[1,1024]{1,0:T(1,128)} %bitcast.15, ...), custom_call_target="tpu_custom_call" | custom-call | tf_op jit(solution)/shard_map/parareal/pallas_call | solution.py:357
  45.3 1.7 %hand_over.1 = (f32[16,1024]{1,0:T(8,128)}, bf16[128,1024]{1,0:T(8,128)(2,1)}) custom-call(f32[16,1024]{1,0:T(8,128)} %get-tuple-element.6.start_in, bf16[128,1024]{1,0:T(8,128)(2,1)} %get-tuple-element.7.wave_in), custom_call_target="tpu_custom_call" | custom-call | tf_op jit(solution)/shard_map/hand_over/pallas_call | solution.py:414
